TPU v7x, 32 devices: a whole 2x2x4 slice. The times are simulated.
32 devices in a mesh: dev: 32 (over z, y, x, core).
Axes of the slice: x: 2, y: 2, z: 4, core: 2. Of those that a mesh axis runs over, the one named last changes fastest.
Arguments:
- dual_blocks: bfloat16 [32, 3072, 3072], P('dev'), as said below
- rigid_modes: float32 [32, 6, 3072], P('dev'), may hold values from -5 to 5
- dual_local: float32 [32, 8, 3072], P('dev'), may hold values from -6 to 6
- coarse_rhs: float32 [32, 6, 8], P('dev'), may hold values from -4608 to 4608
- iface_sizes: int32 [32], P('dev'), may hold values from 1536 to 3072, as said below
- neighbours: int32 [32, 6], P('dev'), may hold values from -1 to 31, as said below
- shared_counts: int32 [32, 6], P('dev'), may hold values from 256 to 512, as said below
- iface_map: int32 [32, 3072], P('dev'), may hold values from -1 to 3071, as said below
- owner: int32 [32], replicated, may hold values from 0 to 31, as said below
Outputs:
- multipliers: float32 [32, 8, 3072], P('dev')
- projected_residual: float32 [32, 8, 3072], P('dev')
Inputs may be any that keep to these rules, and one draw needn't show every extreme that they name: `dual_blocks`: each block is symmetric positive definite, and so is each of its leading principal parts. Grid subdomain g is held by slot owner[g] = (g + s) mod 32 for one offset s of the draw, so the subdomains across the faces -x, +x, -y, +y, -z, +z of slot i sit in slots i - 1, i + 1, i - 4, i + 4, i - 16, i + 16, taken mod 32. `neighbours`: the subdomains form a grid of 4 x 4 x 32/16 with g = x + 4 y + 16 z. Row i lists, for the faces -x, +x, -y, +y, -z, +z of the subdomain held in slot i, the grid subdomain across that face, or -1 on the outer boundary; across a face from g the opposite face names g. `shared_counts`: equal on both sides of a shared face; some subdomain has 512 on all its faces. `iface_sizes`: the sum of the slot's shared_counts row; some subdomain has 3072. `iface_map`: for j < iface_sizes[i], entry j is f * 512 + p for the dof at position p of face f of slot i (p below that face's count), each such code once; -1 beyond. The dof at position p of a shared face pairs with the dof at position p of the opposite face of the neighbour.
All inputs are finite; a program needn't handle non-finite values.
Results may differ from a plain program's by a relative error of at most 0.025.
Values sent between devices are 32-bit elements; how exact they have to be, the bound alone decides.
A program may use at most 128 MiB of HBM per device.

v0:
```python
import jax
import jax.numpy as jnp
from jax import lax
from jax.sharding import PartitionSpec as P

FACES = 6
MODES = 6
CAP = 512
NMAX = 3072
ITERS = 3
HIGHEST_PRECISION = lax.Precision.HIGHEST
OPPOSITE = (1, 0, 3, 2, 5, 4)
FACE_STEPS = (-1, 1, -4, 4, -16, 16)


def from_behind(value, axis, by):
    length = lax.axis_size(axis)
    return lax.ppermute(value, axis, [(i, (i + by) % length) for i in range(length)])


def solve_coarse(factor, vector):
    middle = lax.linalg.triangular_solve(factor, vector, left_side=True, lower=True)
    return lax.linalg.triangular_solve(factor, middle, left_side=True, lower=True, transpose_a=True)


def per_device(
    dual_blocks,
    rigid_modes,
    dual_local,
    coarse_rhs,
    iface_sizes,
    neighbours,
    shared_counts,
    iface_map,
    owner,
):
    my_slot = lax.axis_index("dev")
    devices = lax.axis_size("dev")
    loads = dual_local.shape[1]
    columns = jnp.arange(NMAX, dtype=jnp.int32)
    live_dofs = columns < iface_sizes[0]
    dof_codes = jnp.clip(jnp.where(live_dofs, iface_map[0], 0), 0, FACES * CAP - 1)
    which_face = dof_codes // CAP
    position = dof_codes % CAP
    face_row = neighbours[0]
    count_row = shared_counts[0]
    face_onehot = which_face[None, :] == jnp.arange(FACES, dtype=jnp.int32)[:, None]
    has_partner = jnp.any(face_onehot & (face_row >= 0)[:, None], axis=0)
    face_limit = jnp.sum(jnp.where(face_onehot, count_row[:, None], 0), axis=0)
    shared = live_dofs & has_partner & (position < face_limit)
    live_float = live_dofs.astype(jnp.float32)
    shared_float = shared.astype(jnp.float32)
    weights = jnp.where(shared, 0.5, live_float)
    targets = jnp.where(live_dofs, dof_codes, FACES * CAP)
    inverse = (
        jnp.full((FACES * CAP,), NMAX, jnp.int32)
        .at[targets]
        .set(columns, mode="drop")
        .reshape(FACES, CAP)
    )
    partner_slot = jnp.where(face_row >= 0, owner[jnp.clip(face_row, 0, owner.shape[0] - 1)], 0)
    face_mask = (
        (face_row >= 0)[:, None] & (jnp.arange(CAP, dtype=jnp.int32)[None, :] < count_row[:, None])
    ).astype(jnp.float32)

    def gather_faces(values):
        padded = jnp.concatenate([values, jnp.zeros((values.shape[0], 1), values.dtype)], axis=1)
        return jnp.take(padded, inverse, axis=1)

    def across_faces(face_vals, mover):
        pieces = [mover(face_vals[:, OPPOSITE[face]], -FACE_STEPS[face]) for face in range(FACES)]
        return jnp.stack(pieces, axis=1) * face_mask[None]

    def spread_back(far_faces):
        flattened = far_faces.reshape(far_faces.shape[0], FACES * CAP)
        return jnp.take(flattened, dof_codes, axis=1) * shared_float[None]

    def combine(values, far_faces):
        return live_float[None] * (values - spread_back(far_faces))

    def partial_inner(left_vec, right_vec):
        return jnp.sum(weights[None] * left_vec * right_vec, axis=1)

    modes_live = rigid_modes[0] * live_float[None]
    local_rhs = dual_local[0]
    own_modes = gather_faces(modes_live)
    own_rhs = gather_faces(local_rhs)
    setup_pieces = [
        from_behind(
            (own_modes[:, OPPOSITE[face]], own_rhs[:, OPPOSITE[face]]), "dev", -FACE_STEPS[face]
        )
        for face in range(FACES)
    ]
    far_modes = jnp.stack([piece[0] for piece in setup_pieces], axis=1) * face_mask[None]
    far_rhs = jnp.stack([piece[1] for piece in setup_pieces], axis=1) * face_mask[None]
    dual_rhs = combine(local_rhs, far_rhs)
    diagonal = lax.dot_general(
        modes_live, modes_live, (((1,), (1,)), ((), ())), precision=HIGHEST_PRECISION
    )
    coupling = -jnp.einsum("afp,bfp->afb", own_modes, far_modes, precision=HIGHEST_PRECISION)
    block_row = jnp.zeros((MODES, devices, MODES), jnp.float32).at[:, my_slot, :].set(diagonal)
    block_row = block_row.at[:, partner_slot, :].add(coupling)
    coarse_matrix, coarse_goal = (
        lax.all_gather(block_row.reshape(MODES, devices * MODES), "dev", axis=0, tiled=True),
        lax.all_gather(coarse_rhs[0], "dev", axis=0, tiled=True),
    )
    factor = jnp.linalg.cholesky(coarse_matrix)

    def modes_apply(solution):
        stacked = solution.reshape(devices, MODES, loads)
        own_part = lax.dot_general(
            stacked[my_slot], modes_live, (((0,), (0,)), ((), ())), precision=HIGHEST_PRECISION
        )
        far_part = jnp.einsum(
            "bfp,fbl->lfp", far_modes, stacked[partner_slot], precision=HIGHEST_PRECISION
        )
        return combine(own_part, far_part)

    def project(residual):
        coarse_part = lax.dot_general(
            modes_live, residual, (((1,), (1,)), ((), ())), precision=HIGHEST_PRECISION
        )
        placed = jnp.zeros((devices, MODES, loads), jnp.float32).at[my_slot].set(coarse_part)
        coarse_all = lax.psum(placed, "dev").reshape(devices * MODES, loads)
        solution = solve_coarse(factor, coarse_all)
        projected = residual - modes_apply(solution)
        norm_sq = lax.psum(partial_inner(projected, projected), "dev")
        return (projected, norm_sq)

    def dual_apply(vector):
        products = lax.dot_general(
            vector.astype(jnp.bfloat16),
            dual_blocks[0],
            (((1,), (1,)), ((), ())),
            preferred_element_type=jnp.float32,
        )
        far_part = across_faces(
            gather_faces(products), lambda piece, offset: from_behind(piece, "dev", offset)
        )
        return combine(products, far_part)

    multipliers = modes_apply(solve_coarse(factor, coarse_goal))
    residual = dual_rhs - dual_apply(multipliers)
    projected, norm_sq = project(residual)
    direction = projected
    for step_index in range(ITERS):
        applied = dual_apply(direction)
        curvature = lax.psum(partial_inner(direction, applied), "dev")
        step_size = norm_sq / curvature
        multipliers = multipliers + step_size[:, None] * direction
        residual = residual - step_size[:, None] * applied
        projected, norm_next = project(residual)
        direction = projected + (norm_next / norm_sq)[:, None] * direction
        norm_sq = norm_next
    return (multipliers[None], projected[None])


def solution(mesh):
    return jax.shard_map(
        per_device,
        mesh=mesh,
        in_specs=(
            P("dev", None, None),
            P("dev", None, None),
            P("dev", None, None),
            P("dev", None, None),
            P("dev"),
            P("dev", None),
            P("dev", None),
            P("dev", None),
            P(),
        ),
        out_specs=(P("dev", None, None), P("dev", None, None)),
        check_vma=False,
    )
```

profile of v0, /device:TPU:0, one launch (start us, length us, event | category | flops | bytes accessed | tf_op | source)
XLA Modules:
  0.0 945.2 jit_solution(9198826558787820039)
XLA Ops:
  2.1 11.8 %scatter_custom_fusion = s32[3072]{0:T(1024)S(1)} fusion(s32[3072]{0:T(1024)S(1)} %bitcast.527, s32[3072]{0:T(1024)S(1)} %iota.115, s32[]{:T(128)} %constant.261.clone.1), kind=kCustom, calls=%fused_computation.314 | custom fusion | bytes 12292 | tf_op jit(solution)/shard_map/scatter | solution.py:58
  47.6 36.6 %all-gather = f32[1,192,8]{2,0,1:T(1,128)S(1)} all-gather(f32[1,6,8]{2,0,1:T(1,128)S(1)} %copy-done.67), channel_id=2, replica_groups=mesh['dev'=32] {'dev'}, dimensions={1}, use_global_device_ids=true | all-gather | bytes 6336 | tf_op jit(solution)/shard_map/all_gather | solution.py:105
  104.8 39.5 %all-gather.1 = f32[32,6,192]{2,1,0:T(8,128)S(1)} all-gather(f32[1,6,192]{2,1,0:T(8,128)S(1)} %reshape.887), channel_id=1, replica_groups=mesh['dev'=32] {'dev'}, dimensions={0}, use_global_device_ids=true | all-gather | bytes 152064 | tf_op jit(solution)/shard_map/all_gather | solution.py:104
  144.5 11.7 %cholesky.51 = f32[128,128]{1,0:T(8,128)S(1)} custom-call(f32[128,128]{1,0:T(8,128)S(1)} %cholesky.124), custom_call_target="Cholesky" | custom-call | tf_op jit(solution)/shard_map/jit(cholesky)/cholesky | solution.py:107
  175.0 19.8 %custom-call.27 = f32[2,128,128]{1,2,0:T(8,128)S(1)} custom-call(f32[2,128,128]{2,1,0:T(8,128)S(1)} %pad_maximum_fusion), custom_call_target="InvertDiagBlocksLowerTriangular" | custom-call | tf_op jit(solution)/shard_map/triangular_solve/custom-call.4 | solution.py:23
  212.9 12.0 %fusion.6 = f32[8,3072]{1,0:T(8,128)} fusion(bf16[1,3072,3072]{2,1,0:T(8,128)(2,1)} %param.27, f32[8,3072]{1,0:T(8,128)S(1)} %fusion.17), kind=kOutput, calls=%fused_computation.30 | convolution fusion | flops 151019520 | bytes 19070976 | tf_op jit(solution)/shard_map/dot_general | solution.py:131
  277.0 12.6 %gather_fusion.11 = f32[3072,8]{1,0:T(8,128)} fusion(f32[8,3072]{0,1:T(8,128)} %get-tuple-element.205, s32[3072]{0:T(1024)S(1)} %get-tuple-element.216), kind=kCustom, calls=%fused_computation.3.clone | custom fusion | bytes 208896 | tf_op jit(solution)/shard_map/jit(_take)/gather | solution.py:76
  309.1 37.8 %psum.70 = f32[192,8]{0,1:T(8,128)S(1)} all-reduce(f32[192,8]{0,1:T(8,128)S(1)} %reshape.519), channel_id=1, replica_groups=mesh['dev'=32] {'dev'}, use_global_device_ids=true, to_apply=%region_10.15 | all-reduce | flops 1536 | bytes 12288 | tf_op jit(solution)/shard_map/psum | solution.py:124
  366.6 12.0 %fusion.4 = f32[8,3072]{1,0:T(8,128)} fusion(bf16[1,3072,3072]{2,1,0:T(8,128)(2,1)} %param.27, f32[8,3072]{1,0:T(8,128)S(1)} %fusion.16), kind=kOutput, calls=%fused_computation.28 | convolution fusion | flops 151019520 | bytes 19070976 | tf_op jit(solution)/shard_map/dot_general | solution.py:131
  381.3 11.0 %gather_fusion.13 = f32[3072,8]{1,0:T(8,128)S(1)} fusion(f32[8,3073]{0,1:T(8,128)} %concatenate.55.clone, s32[3072]{0:T(1024)} %copy-done.45), kind=kCustom, calls=%fused_computation.12.clone | custom fusion | bytes 208896 | tf_op jit(solution)/shard_map/jit(_take)/gather | solution.py:68
  414.7 13.8 %gather_fusion.14 = f32[3072,8]{1,0:T(8,128)} fusion(f32[8,3072]{0,1:T(8,128)} %bitcast_multiply_fusion.2, s32[3072]{0:T(1024)} %copy-done.34), kind=kCustom, calls=%fused_computation.5.clone | custom fusion | bytes 208896 | tf_op jit(solution)/shard_map/jit(_take)/gather | solution.py:76
  430.6 38.5 %all-reduce.11 = (f32[8]{0:T(128)S(1)}, f32[8]{0:T(128)S(1)}) all-reduce(f32[8]{0:T(128)S(1)} %get-tuple-element.155, f32[8]{0:T(128)S(1)} %get-tuple-element.154), channel_id=1, replica_groups=mesh['dev'=32] {'dev'}, use_global_device_ids=true, to_apply=%region_12.17 | all-reduce | flops 16 | bytes 128 | tf_op jit(solution)/shard_map/psum | solution.py:127
  473.3 39.3 %psum.73 = f32[192,8]{0,1:T(8,128)S(1)} all-reduce(f32[192,8]{0,1:T(8,128)S(1)} %reshape.523), channel_id=1, replica_groups=mesh['dev'=32] {'dev'}, use_global_device_ids=true, to_apply=%region_15.20 | all-reduce | flops 1536 | bytes 12288 | tf_op jit(solution)/shard_map/psum | solution.py:124
  531.8 40.7 %psum.74 = f32[8]{0:T(128)S(1)} all-reduce(f32[8]{0:T(128)S(1)} %get-tuple-element.210), channel_id=1, replica_groups=mesh['dev'=32] {'dev'}, use_global_device_ids=true, to_apply=%region_17.22 | all-reduce | flops 8 | bytes 64 | tf_op jit(solution)/shard_map/psum | solution.py:127
  573.2 12.0 %fusion.2 = f32[8,3072]{1,0:T(8,128)} fusion(bf16[1,3072,3072]{2,1,0:T(8,128)(2,1)} %param.27, f32[8,3072]{1,0:T(8,128)S(1)} %multiply_add_fusion.1), kind=kOutput, calls=%fused_computation.26 | convolution fusion | flops 151019520 | bytes 19070976 | tf_op jit(solution)/shard_map/dot_general | solution.py:131
  621.4 13.4 %gather_fusion.17 = f32[3072,8]{1,0:T(8,128)} fusion(f32[8,3072]{0,1:T(8,128)} %bitcast_multiply_fusion.1, s32[3072]{0:T(1024)} %copy-done.34), kind=kCustom, calls=%fused_computation.7.clone | custom fusion | bytes 208896 | tf_op jit(solution)/shard_map/jit(_take)/gather | solution.py:76
  636.8 38.5 %psum.75 = f32[8]{0:T(128)S(1)} all-reduce(f32[8]{0:T(128)S(1)} %multiply_reduce_fusion.1), channel_id=1, replica_groups=mesh['dev'=32] {'dev'}, use_global_device_ids=true, to_apply=%region_19.24 | all-reduce | flops 8 | bytes 64 | tf_op jit(solution)/shard_map/psum | solution.py:148
  679.7 39.3 %psum.76 = f32[192,8]{0,1:T(8,128)S(1)} all-reduce(f32[192,8]{0,1:T(8,128)S(1)} %reshape.527), channel_id=1, replica_groups=mesh['dev'=32] {'dev'}, use_global_device_ids=true, to_apply=%region_20.25 | all-reduce | flops 1536 | bytes 12288 | tf_op jit(solution)/shard_map/psum | solution.py:124
  725.5 11.9 %gather_fusion.18 = f32[3072,8]{1,0:T(8,128)} fusion(f32[8,3072]{0,1:T(8,128)S(1)} %copy.177, s32[3072]{0:T(1024)} %copy-done.34), kind=kCustom, calls=%fused_computation.8.clone | custom fusion | bytes 208896 | tf_op jit(solution)/shard_map/jit(_take)/gather | solution.py:76
  739.8 40.8 %psum.77 = f32[8]{0:T(128)S(1)} all-reduce(f32[8]{0:T(128)S(1)} %get-tuple-element.212), channel_id=1, replica_groups=mesh['dev'=32] {'dev'}, use_global_device_ids=true, to_apply=%region_22.27 | all-reduce | flops 8 | bytes 64 | tf_op jit(solution)/shard_map/psum | solution.py:127
  781.1 12.0 %fusion = f32[8,3072]{1,0:T(8,128)} fusion(bf16[1,3072,3072]{2,1,0:T(8,128)(2,1)} %param.27, f32[8,3072]{1,0:T(8,128)S(1)} %get-tuple-element.213, f32[8,3072]{1,0:T(8,128)S(1)} %multiply_add_fusion.1, f32[8]{0:T(128)S(1)} %div.44), kind=kOutput, calls=%fused_computation.24 | convolution fusion | flops 151068672 | bytes 19169312 | tf_op jit(solution)/shard_map/dot_general | solution.py:131
  829.2 13.5 %gather_fusion.20 = f32[3072,8]{1,0:T(8,128)} fusion(f32[8,3072]{0,1:T(8,128)} %bitcast_multiply_fusion, s32[3072]{0:T(1024)} %copy-done.34), kind=kCustom, calls=%fused_computation.9.clone | custom fusion | bytes 208896 | tf_op jit(solution)/shard_map/jit(_take)/gather | solution.py:76
  844.8 38.5 %psum.78 = f32[8]{0:T(128)S(1)} all-reduce(f32[8]{0:T(128)S(1)} %get-tuple-element.158), channel_id=1, replica_groups=mesh['dev'=32] {'dev'}, use_global_device_ids=true, to_apply=%region_24.29 | all-reduce | flops 8 | bytes 64 | tf_op jit(solution)/shard_map/psum | solution.py:148
  887.6 39.3 %psum.79 = f32[192,8]{0,1:T(8,128)S(1)} all-reduce(f32[192,8]{0,1:T(8,128)S(1)} %reshape.531), channel_id=1, replica_groups=mesh['dev'=32] {'dev'}, use_global_device_ids=true, to_apply=%region_25.30 | all-reduce | flops 1536 | bytes 12288 | tf_op jit(solution)/shard_map/psum | solution.py:124
  (495 shorter events, 344.6 us)
Async XLA Ops:
  29.5 67.2 %collective-permute-start = (f32[6,512]{1,0:T(8,128)}, f32[6,512]{1,0:T(8,128)}, u32[]{:S(2)}, u32[]{:S(2)}) collective-permute-start(f32[6,512]{1,0:T(8,128)} %get-tuple-element.199), channel_id=1, source_target_pairs={{0,1},{1,2},{2,3},{3,4},{4,5},{5,6},{6,7},{7,8},{8,9},{9,10},{10,1... | collective-permute-start | bytes 36872 | tf_op jit(solution)/shard_map/ppermute | solution.py:18
  30.0 67.4 %collective-permute-start.1 = (f32[6,512]{1,0:T(8,128)}, f32[6,512]{1,0:T(8,128)}, u32[]{:S(2)}, u32[]{:S(2)}) collective-permute-start(f32[6,512]{1,0:T(8,128)} %get-tuple-element.198), channel_id=1, source_target_pairs={{0,31},{1,0},{2,1},{3,2},{4,3},{5,4},{6,5},{7,6},{8,7},{9,8},{10,9... | collective-permute-start | bytes 36872 | tf_op jit(solution)/shard_map/ppermute | solution.py:18
  36.0 62.2 %collective-permute-start.2 = (f32[6,512]{1,0:T(8,128)}, f32[6,512]{1,0:T(8,128)}, u32[]{:S(2)}, u32[]{:S(2)}) collective-permute-start(f32[6,512]{1,0:T(8,128)} %get-tuple-element.197), channel_id=1, source_target_pairs={{0,4},{1,5},{2,6},{3,7},{4,8},{5,9},{6,10},{7,11},{8,12},{9,13},{1... | collective-permute-start | bytes 36872 | tf_op jit(solution)/shard_map/ppermute | solution.py:18
  36.0 62.9 %collective-permute-start.3 = (f32[6,512]{1,0:T(8,128)}, f32[6,512]{1,0:T(8,128)}, u32[]{:S(2)}, u32[]{:S(2)}) collective-permute-start(f32[6,512]{1,0:T(8,128)} %get-tuple-element.196), channel_id=1, source_target_pairs={{0,28},{1,29},{2,30},{3,31},{4,0},{5,1},{6,2},{7,3},{8,4},{9,5},{1... | collective-permute-start | bytes 36872 | tf_op jit(solution)/shard_map/ppermute | solution.py:18
  40.7 58.9 %collective-permute-start.4 = (f32[6,512]{1,0:T(8,128)}, f32[6,512]{1,0:T(8,128)}, u32[]{:S(2)}, u32[]{:S(2)}) collective-permute-start(f32[6,512]{1,0:T(8,128)} %get-tuple-element.195), channel_id=1, source_target_pairs={{0,16},{1,17},{2,18},{3,19},{4,20},{5,21},{6,22},{7,23},{8,24},{9,... | collective-permute-start | bytes 36872 | tf_op jit(solution)/shard_map/ppermute | solution.py:18
  239.2 10.1 %collective-permute-start.6 = (f32[8,512]{1,0:T(8,128)S(1)}, f32[8,512]{1,0:T(8,128)S(1)}, u32[]{:S(2)}, u32[]{:S(2)}) collective-permute-start(f32[8,512]{1,0:T(8,128)S(1)} %get-tuple-element.187), channel_id=1, source_target_pairs={{0,1},{1,2},{2,3},{3,4},{4,5},{5,6},{6,7},{7,8},{8,9},{9,10},{10,1... | collective-permute-start | bytes 49160 | tf_op jit(solution)/shard_map/ppermute | solution.py:18
  239.6 18.3 %collective-permute-start.7 = (f32[8,512]{1,0:T(8,128)S(1)}, f32[8,512]{1,0:T(8,128)S(1)}, u32[]{:S(2)}, u32[]{:S(2)}) collective-permute-start(f32[8,512]{1,0:T(8,128)S(1)} %get-tuple-element.186), channel_id=1, source_target_pairs={{0,31},{1,0},{2,1},{3,2},{4,3},{5,4},{6,5},{7,6},{8,7},{9,8},{10,9... | collective-permute-start | bytes 49160 | tf_op jit(solution)/shard_map/ppermute | solution.py:18
  244.6 13.4 %collective-permute-start.8 = (f32[8,512]{1,0:T(8,128)S(1)}, f32[8,512]{1,0:T(8,128)S(1)}, u32[]{:S(2)}, u32[]{:S(2)}) collective-permute-start(f32[8,512]{1,0:T(8,128)S(1)} %get-tuple-element.185), channel_id=1, source_target_pairs={{0,4},{1,5},{2,6},{3,7},{4,8},{5,9},{6,10},{7,11},{8,12},{9,13},{1... | collective-permute-start | bytes 49160 | tf_op jit(solution)/shard_map/ppermute | solution.py:18
  244.6 13.4 %collective-permute-start.9 = (f32[8,512]{1,0:T(8,128)S(1)}, f32[8,512]{1,0:T(8,128)S(1)}, u32[]{:S(2)}, u32[]{:S(2)}) collective-permute-start(f32[8,512]{1,0:T(8,128)S(1)} %get-tuple-element.184), channel_id=1, source_target_pairs={{0,28},{1,29},{2,30},{3,31},{4,0},{5,1},{6,2},{7,3},{8,4},{9,5},{1... | collective-permute-start | bytes 49160 | tf_op jit(solution)/shard_map/ppermute | solution.py:18
  249.3 13.4 %collective-permute-start.10 = (f32[8,512]{1,0:T(8,128)S(1)}, f32[8,512]{1,0:T(8,128)S(1)}, u32[]{:S(2)}, u32[]{:S(2)}) collective-permute-start(f32[8,512]{1,0:T(8,128)S(1)} %get-tuple-element.183), channel_id=1, source_target_pairs={{0,16},{1,17},{2,18},{3,19},{4,20},{5,21},{6,22},{7,23},{8,24},{9,... | collective-permute-start | bytes 49160 | tf_op jit(solution)/shard_map/ppermute | solution.py:18
  257.9 8.3 collective-permute-start.14
  258.0 8.9 collective-permute-start.15
  394.3 10.1 %collective-permute-start.18 = (f32[8,512]{1,0:T(8,128)S(1)}, f32[8,512]{1,0:T(8,128)S(1)}, u32[]{:S(2)}, u32[]{:S(2)}) collective-permute-start(f32[8,512]{1,0:T(8,128)S(1)} %get-tuple-element.181), channel_id=1, source_target_pairs={{0,1},{1,2},{2,3},{3,4},{4,5},{5,6},{6,7},{7,8},{8,9},{9,10},{10,1... | collective-permute-start | bytes 49160 | tf_op jit(solution)/shard_map/ppermute | solution.py:18
  394.4 13.6 %collective-permute-start.19 = (f32[8,512]{1,0:T(8,128)S(1)}, f32[8,512]{1,0:T(8,128)S(1)}, u32[]{:S(2)}, u32[]{:S(2)}) collective-permute-start(f32[8,512]{1,0:T(8,128)S(1)} %get-tuple-element.180), channel_id=1, source_target_pairs={{0,31},{1,0},{2,1},{3,2},{4,3},{5,4},{6,5},{7,6},{8,7},{9,8},{10,9... | collective-permute-start | bytes 49160 | tf_op jit(solution)/shard_map/ppermute | solution.py:18
  399.7 8.9 collective-permute-start.20
  399.7 9.5 %collective-permute-start.21 = (f32[8,512]{1,0:T(8,128)S(1)}, f32[8,512]{1,0:T(8,128)S(1)}, u32[]{:S(2)}, u32[]{:S(2)}) collective-permute-start(f32[8,512]{1,0:T(8,128)S(1)} %get-tuple-element.178), channel_id=1, source_target_pairs={{0,28},{1,29},{2,30},{3,31},{4,0},{5,1},{6,2},{7,3},{8,4},{9,5},{1... | collective-permute-start | bytes 49160 | tf_op jit(solution)/shard_map/ppermute | solution.py:18
  600.8 10.3 %collective-permute-start.24 = (f32[8,512]{1,0:T(8,128)S(1)}, f32[8,512]{1,0:T(8,128)S(1)}, u32[]{:S(2)}, u32[]{:S(2)}) collective-permute-start(f32[8,512]{1,0:T(8,128)S(1)} %get-tuple-element.175), channel_id=1, source_target_pairs={{0,1},{1,2},{2,3},{3,4},{4,5},{5,6},{6,7},{7,8},{8,9},{9,10},{10,1... | collective-permute-start | bytes 49160 | tf_op jit(solution)/shard_map/ppermute | solution.py:18
  600.9 13.7 %collective-permute-start.25 = (f32[8,512]{1,0:T(8,128)S(1)}, f32[8,512]{1,0:T(8,128)S(1)}, u32[]{:S(2)}, u32[]{:S(2)}) collective-permute-start(f32[8,512]{1,0:T(8,128)S(1)} %get-tuple-element.174), channel_id=1, source_target_pairs={{0,31},{1,0},{2,1},{3,2},{4,3},{5,4},{6,5},{7,6},{8,7},{9,8},{10,9... | collective-permute-start | bytes 49160 | tf_op jit(solution)/shard_map/ppermute | solution.py:18
  606.2 9.0 collective-permute-start.26
  606.2 9.6 %collective-permute-start.27 = (f32[8,512]{1,0:T(8,128)S(1)}, f32[8,512]{1,0:T(8,128)S(1)}, u32[]{:S(2)}, u32[]{:S(2)}) collective-permute-start(f32[8,512]{1,0:T(8,128)S(1)} %get-tuple-element.172), channel_id=1, source_target_pairs={{0,28},{1,29},{2,30},{3,31},{4,0},{5,1},{6,2},{7,3},{8,4},{9,5},{1... | collective-permute-start | bytes 49160 | tf_op jit(solution)/shard_map/ppermute | solution.py:18
  808.7 10.1 %collective-permute-start.30 = (f32[8,512]{1,0:T(8,128)S(1)}, f32[8,512]{1,0:T(8,128)S(1)}, u32[]{:S(2)}, u32[]{:S(2)}) collective-permute-start(f32[8,512]{1,0:T(8,128)S(1)} %get-tuple-element.169), channel_id=1, source_target_pairs={{0,1},{1,2},{2,3},{3,4},{4,5},{5,6},{6,7},{7,8},{8,9},{9,10},{10,1... | collective-permute-start | bytes 49160 | tf_op jit(solution)/shard_map/ppermute | solution.py:18
  808.8 13.6 %collective-permute-start.31 = (f32[8,512]{1,0:T(8,128)S(1)}, f32[8,512]{1,0:T(8,128)S(1)}, u32[]{:S(2)}, u32[]{:S(2)}) collective-permute-start(f32[8,512]{1,0:T(8,128)S(1)} %get-tuple-element.168), channel_id=1, source_target_pairs={{0,31},{1,0},{2,1},{3,2},{4,3},{5,4},{6,5},{7,6},{8,7},{9,8},{10,9... | collective-permute-start | bytes 49160 | tf_op jit(solution)/shard_map/ppermute | solution.py:18
  814.1 8.9 collective-permute-start.32
  814.1 9.5 %collective-permute-start.33 = (f32[8,512]{1,0:T(8,128)S(1)}, f32[8,512]{1,0:T(8,128)S(1)}, u32[]{:S(2)}, u32[]{:S(2)}) collective-permute-start(f32[8,512]{1,0:T(8,128)S(1)} %get-tuple-element.166), channel_id=1, source_target_pairs={{0,28},{1,29},{2,30},{3,31},{4,0},{5,1},{6,2},{7,3},{8,4},{9,5},{1... | collective-permute-start | bytes 49160 | tf_op jit(solution)/shard_map/ppermute | solution.py:18
  (94 other events, 3324.5 us)
where the time goes:
time: 954 us; the launch traced here: 945 us
  blocking collectives  429 us (45%)
  local copies, waits for them, and re-layouts  283 us (30%)
  matrix products  80.1 us (8%)
  other arithmetic  72 us (8%)
  starting transfers between devices  69.4 us (7%)
    psum x4, blocking collectives, project(): coarse_all = lax.psum(placed, 'dev').reshape(devices * MODES, loads)  156 us
    gather x20, local copies, waits for them, and re-layouts, spread_back(): return jnp.take(flattened, dof_codes, axis=1) * shared_float[None]  139 us
    psum x3, blocking collectives, project(): norm_sq = lax.psum(partial_inner(projected, projected), 'dev')  120 us
    psum x2, blocking collectives, per_device(): curvature = lax.psum(partial_inner(direction, applied), 'dev')  77 us
    gather x12, local copies, waits for them, and re-layouts, gather_faces(): return jnp.take(padded, inverse, axis=1)  70.2 us
    ppermute x36, starting transfers between devices, from_behind(): lax.ppermute(value, axis, [(i, (i + by) % length) for i in range(length)])  69.4 us
    dot_general x4, matrix products, dual_apply(): lax.dot_general(vector.astype(jnp.bfloat16), dual_blocks[0], (((1,), (1,)...  47.9 us
    all_gather x1, blocking collectives, per_device(): lax.all_gather(block_row.reshape(MODES, devices * MODES), 'dev', axis=0,...  39.5 us
  transfers between devices with their start and end apart: 36, of which 2 were waited for; matrix products, arithmetic and copies ran while one was open for 4% of the time, Pallas kernels for 0%

commit v1 on v0

--- a/solution.py
+++ b/solution.py
@@ -124,7 +124,9 @@
         coarse_all = lax.psum(placed, "dev").reshape(devices * MODES, loads)
         solution = solve_coarse(factor, coarse_all)
         projected = residual - modes_apply(solution)
-        norm_sq = lax.psum(partial_inner(projected, projected), "dev")
+        block = partial_inner(projected, projected)
+        parts = lax.all_gather(block, "dev")
+        norm_sq = jnp.sum(parts, axis=0)
         return (projected, norm_sq)
 
     def dual_apply(vector):

time: 954 us -> 955 us (level)
    psum x3 -> x0, blocking collectives: 120 us -> none  [project(): norm_sq = lax.psum(partial_inner(projected, projected), 'dev')]
    unnamed x0 -> x3, blocking collectives: none -> 120 us
    unnamed x203 -> x209, local copies, waits for them, and re-layouts: 27.1 us -> 27.7 us
where the time goes in v1:
time: 955 us; the launch traced here: 946 us
  blocking collectives  429 us (45%)
  local copies, waits for them, and re-layouts  283 us (30%)
  matrix products  80.5 us (8%)
  other arithmetic  72.2 us (8%)
  starting transfers between devices  69.4 us (7%)
    psum x4, blocking collectives, project(): coarse_all = lax.psum(placed, 'dev').reshape(devices * MODES, loads)  156 us
    gather x20, local copies, waits for them, and re-layouts, spread_back(): return jnp.take(flattened, dof_codes, axis=1) * shared_float[None]  138 us
    unnamed x3, blocking collectives  120 us
    psum x2, blocking collectives, per_device(): curvature = lax.psum(partial_inner(direction, applied), 'dev')  77 us
    gather x12, local copies, waits for them, and re-layouts, gather_faces(): return jnp.take(padded, inverse, axis=1)  70.2 us
    ppermute x36, starting transfers between devices, from_behind(): lax.ppermute(value, axis, [(i, (i + by) % length) for i in range(length)])  69.4 us
    dot_general x4, matrix products, dual_apply(): lax.dot_general(vector.astype(jnp.bfloat16), dual_blocks[0], (((1,), (1,)...  48 us
    all_gather x1, blocking collectives, per_device(): lax.all_gather(block_row.reshape(MODES, devices * MODES), 'dev', axis=0,...  39.5 us
  transfers between devices with their start and end apart: 36, of which 2 were waited for; matrix products, arithmetic and copies ran while one was open for 4% of the time, Pallas kernels for 0%

profile of v1, /device:TPU:0, one launch (start us, length us, event | category | flops | bytes accessed | tf_op | source)
XLA Modules:
  0.0 946.2 jit_solution(17464302292947022002)
XLA Ops:
  2.1 11.8 %scatter_custom_fusion = s32[3072]{0:T(1024)S(1)} fusion(s32[3072]{0:T(1024)S(1)} %bitcast.527, s32[3072]{0:T(1024)S(1)} %iota.115, s32[]{:T(128)} %constant.261.clone.1), kind=kCustom, calls=%fused_computation.314 | custom fusion | bytes 12292 | tf_op jit(solution)/shard_map/scatter | solution.py:58
  47.8 36.6 %all-gather = f32[1,192,8]{2,0,1:T(1,128)S(1)} all-gather(f32[1,6,8]{2,0,1:T(1,128)S(1)} %copy-done.67), channel_id=2, replica_groups=mesh['dev'=32] {'dev'}, dimensions={1}, use_global_device_ids=true | all-gather | bytes 6336 | tf_op jit(solution)/shard_map/all_gather | solution.py:105
  104.9 39.5 %all-gather.4 = f32[32,6,192]{2,1,0:T(8,128)S(1)} all-gather(f32[1,6,192]{2,1,0:T(8,128)S(1)} %reshape.904), channel_id=1, replica_groups=mesh['dev'=32] {'dev'}, dimensions={0}, use_global_device_ids=true | all-gather | bytes 152064 | tf_op jit(solution)/shard_map/all_gather | solution.py:104
  144.6 11.7 %cholesky.51 = f32[128,128]{1,0:T(8,128)S(1)} custom-call(f32[128,128]{1,0:T(8,128)S(1)} %cholesky.124), custom_call_target="Cholesky" | custom-call | tf_op jit(solution)/shard_map/jit(cholesky)/cholesky | solution.py:107
  175.3 19.8 %custom-call.27 = f32[2,128,128]{1,2,0:T(8,128)S(1)} custom-call(f32[2,128,128]{2,1,0:T(8,128)S(1)} %pad_maximum_fusion), custom_call_target="InvertDiagBlocksLowerTriangular" | custom-call | tf_op jit(solution)/shard_map/triangular_solve/custom-call.4 | solution.py:23
  213.2 12.0 %fusion.6 = f32[8,3072]{1,0:T(8,128)} fusion(bf16[1,3072,3072]{2,1,0:T(8,128)(2,1)} %param.27, f32[8,3072]{1,0:T(8,128)S(1)} %fusion.17), kind=kOutput, calls=%fused_computation.30 | convolution fusion | flops 151019520 | bytes 19070976 | tf_op jit(solution)/shard_map/dot_general | solution.py:133
  277.2 12.6 %gather_fusion.11 = f32[3072,8]{1,0:T(8,128)} fusion(f32[8,3072]{0,1:T(8,128)} %get-tuple-element.205, s32[3072]{0:T(1024)S(1)} %get-tuple-element.216), kind=kCustom, calls=%fused_computation.3.clone | custom fusion | bytes 208896 | tf_op jit(solution)/shard_map/jit(_take)/gather | solution.py:76
  309.3 37.9 %psum.49 = f32[192,8]{0,1:T(8,128)S(1)} all-reduce(f32[192,8]{0,1:T(8,128)S(1)} %reshape.527), channel_id=1, replica_groups=mesh['dev'=32] {'dev'}, use_global_device_ids=true, to_apply=%region_10.15 | all-reduce | flops 1536 | bytes 12288 | tf_op jit(solution)/shard_map/psum | solution.py:124
  366.7 12.0 %fusion.4 = f32[8,3072]{1,0:T(8,128)} fusion(bf16[1,3072,3072]{2,1,0:T(8,128)(2,1)} %param.27, f32[8,3072]{1,0:T(8,128)S(1)} %fusion.16), kind=kOutput, calls=%fused_computation.28 | convolution fusion | flops 151019520 | bytes 19070976 | tf_op jit(solution)/shard_map/dot_general | solution.py:133
  414.8 13.7 %gather_fusion.14 = f32[3072,8]{1,0:T(8,128)} fusion(f32[8,3072]{0,1:T(8,128)} %bitcast_multiply_fusion.2, s32[3072]{0:T(1024)} %copy-done.34), kind=kCustom, calls=%fused_computation.5.clone | custom fusion | bytes 208896 | tf_op jit(solution)/shard_map/jit(_take)/gather | solution.py:76
  430.8 38.4 %all-reduce.14 = (f32[256]{0:T(256)S(1)}, f32[8]{0:T(128)S(1)}) all-reduce(f32[256]{0:T(256)S(1)} %dynamic-update-slice.26, f32[8]{0:T(128)S(1)} %get-tuple-element.154), channel_id=3, replica_groups=mesh['dev'=32] {'dev'}, use_global_device_ids=true, to_apply=%add.11 | all-reduce | flops 264 | bytes 2112
  473.6 39.3 %psum.51 = f32[192,8]{0,1:T(8,128)S(1)} all-reduce(f32[192,8]{0,1:T(8,128)S(1)} %reshape.531), channel_id=1, replica_groups=mesh['dev'=32] {'dev'}, use_global_device_ids=true, to_apply=%region_15.20 | all-reduce | flops 1536 | bytes 12288 | tf_op jit(solution)/shard_map/psum | solution.py:124
  532.3 40.7 %all-reduce.12 = f32[256]{0:T(256)S(1)} all-reduce(f32[256]{0:T(256)S(1)} %dynamic-update-slice.27), channel_id=4, replica_groups=mesh['dev'=32] {'dev'}, use_global_device_ids=true, to_apply=%add.12 | all-reduce | flops 256 | bytes 2048
  573.7 12.0 %fusion.2 = f32[8,3072]{1,0:T(8,128)} fusion(bf16[1,3072,3072]{2,1,0:T(8,128)(2,1)} %param.27, f32[8,3072]{1,0:T(8,128)S(1)} %multiply_add_fusion.1), kind=kOutput, calls=%fused_computation.26 | convolution fusion | flops 151019520 | bytes 19070976 | tf_op jit(solution)/shard_map/dot_general | solution.py:133
  588.3 11.0 %gather_fusion.16 = f32[3072,8]{1,0:T(8,128)S(1)} fusion(f32[8,3073]{0,1:T(8,128)} %concatenate.56.clone, s32[3072]{0:T(1024)} %copy-done.45), kind=kCustom, calls=%fused_computation.13.clone | custom fusion | bytes 208896 | tf_op jit(solution)/shard_map/jit(_take)/gather | solution.py:68
  621.9 13.4 %gather_fusion.17 = f32[3072,8]{1,0:T(8,128)} fusion(f32[8,3072]{0,1:T(8,128)} %bitcast_multiply_fusion.1, s32[3072]{0:T(1024)} %copy-done.34), kind=kCustom, calls=%fused_computation.7.clone | custom fusion | bytes 208896 | tf_op jit(solution)/shard_map/jit(_take)/gather | solution.py:76
  637.3 38.5 %psum.52 = f32[8]{0:T(128)S(1)} all-reduce(f32[8]{0:T(128)S(1)} %multiply_reduce_fusion.1), channel_id=1, replica_groups=mesh['dev'=32] {'dev'}, use_global_device_ids=true, to_apply=%region_19.24 | all-reduce | flops 8 | bytes 64 | tf_op jit(solution)/shard_map/psum | solution.py:150
  680.1 39.3 %psum.53 = f32[192,8]{0,1:T(8,128)S(1)} all-reduce(f32[192,8]{0,1:T(8,128)S(1)} %reshape.535), channel_id=1, replica_groups=mesh['dev'=32] {'dev'}, use_global_device_ids=true, to_apply=%region_20.25 | all-reduce | flops 1536 | bytes 12288 | tf_op jit(solution)/shard_map/psum | solution.py:124
  726.0 11.8 %gather_fusion.18 = f32[3072,8]{1,0:T(8,128)} fusion(f32[8,3072]{0,1:T(8,128)S(1)} %copy.177, s32[3072]{0:T(1024)} %copy-done.34), kind=kCustom, calls=%fused_computation.8.clone | custom fusion | bytes 208896 | tf_op jit(solution)/shard_map/jit(_take)/gather | solution.py:76
  740.5 40.9 %all-reduce.13 = f32[256]{0:T(256)S(1)} all-reduce(f32[256]{0:T(256)S(1)} %dynamic-update-slice.28), channel_id=5, replica_groups=mesh['dev'=32] {'dev'}, use_global_device_ids=true, to_apply=%add.13 | all-reduce | flops 256 | bytes 2048
  782.1 12.0 %fusion = f32[8,3072]{1,0:T(8,128)} fusion(bf16[1,3072,3072]{2,1,0:T(8,128)(2,1)} %param.27, f32[8,3072]{1,0:T(8,128)S(1)} %get-tuple-element.213, f32[8,3072]{1,0:T(8,128)S(1)} %multiply_add_fusion.1, f32[8]{0:T(128)S(1)} %div.52), kind=kOutput, calls=%fused_computation.24 | convolution fusion | flops 151068672 | bytes 19169312 | tf_op jit(solution)/shard_map/dot_general | solution.py:133
  830.2 13.4 %gather_fusion.20 = f32[3072,8]{1,0:T(8,128)} fusion(f32[8,3072]{0,1:T(8,128)} %bitcast_multiply_fusion, s32[3072]{0:T(1024)} %copy-done.34), kind=kCustom, calls=%fused_computation.9.clone | custom fusion | bytes 208896 | tf_op jit(solution)/shard_map/jit(_take)/gather | solution.py:76
  845.7 38.5 %psum.54 = f32[8]{0:T(128)S(1)} all-reduce(f32[8]{0:T(128)S(1)} %get-tuple-element.158), channel_id=1, replica_groups=mesh['dev'=32] {'dev'}, use_global_device_ids=true, to_apply=%region_24.29 | all-reduce | flops 8 | bytes 64 | tf_op jit(solution)/shard_map/psum | solution.py:150
  888.6 39.3 %psum.55 = f32[192,8]{0,1:T(8,128)S(1)} all-reduce(f32[192,8]{0,1:T(8,128)S(1)} %reshape.539), channel_id=1, replica_groups=mesh['dev'=32] {'dev'}, use_global_device_ids=true, to_apply=%region_25.30 | all-reduce | flops 1536 | bytes 12288 | tf_op jit(solution)/shard_map/psum | solution.py:124
  (507 shorter events, 345.6 us)
Async XLA Ops:
  29.5 67.4 %collective-permute-start = (f32[6,512]{1,0:T(8,128)}, f32[6,512]{1,0:T(8,128)}, u32[]{:S(2)}, u32[]{:S(2)}) collective-permute-start(f32[6,512]{1,0:T(8,128)} %get-tuple-element.199), channel_id=1, source_target_pairs={{0,1},{1,2},{2,3},{3,4},{4,5},{5,6},{6,7},{7,8},{8,9},{9,10},{10,1... | collective-permute-start | bytes 36872 | tf_op jit(solution)/shard_map/ppermute | solution.py:18
  30.0 67.6 %collective-permute-start.1 = (f32[6,512]{1,0:T(8,128)}, f32[6,512]{1,0:T(8,128)}, u32[]{:S(2)}, u32[]{:S(2)}) collective-permute-start(f32[6,512]{1,0:T(8,128)} %get-tuple-element.198), channel_id=1, source_target_pairs={{0,31},{1,0},{2,1},{3,2},{4,3},{5,4},{6,5},{7,6},{8,7},{9,8},{10,9... | collective-permute-start | bytes 36872 | tf_op jit(solution)/shard_map/ppermute | solution.py:18
  35.9 62.4 %collective-permute-start.2 = (f32[6,512]{1,0:T(8,128)}, f32[6,512]{1,0:T(8,128)}, u32[]{:S(2)}, u32[]{:S(2)}) collective-permute-start(f32[6,512]{1,0:T(8,128)} %get-tuple-element.197), channel_id=1, source_target_pairs={{0,4},{1,5},{2,6},{3,7},{4,8},{5,9},{6,10},{7,11},{8,12},{9,13},{1... | collective-permute-start | bytes 36872 | tf_op jit(solution)/shard_map/ppermute | solution.py:18
  35.9 63.1 %collective-permute-start.3 = (f32[6,512]{1,0:T(8,128)}, f32[6,512]{1,0:T(8,128)}, u32[]{:S(2)}, u32[]{:S(2)}) collective-permute-start(f32[6,512]{1,0:T(8,128)} %get-tuple-element.196), channel_id=1, source_target_pairs={{0,28},{1,29},{2,30},{3,31},{4,0},{5,1},{6,2},{7,3},{8,4},{9,5},{1... | collective-permute-start | bytes 36872 | tf_op jit(solution)/shard_map/ppermute | solution.py:18
  40.6 59.1 %collective-permute-start.4 = (f32[6,512]{1,0:T(8,128)}, f32[6,512]{1,0:T(8,128)}, u32[]{:S(2)}, u32[]{:S(2)}) collective-permute-start(f32[6,512]{1,0:T(8,128)} %get-tuple-element.195), channel_id=1, source_target_pairs={{0,16},{1,17},{2,18},{3,19},{4,20},{5,21},{6,22},{7,23},{8,24},{9,... | collective-permute-start | bytes 36872 | tf_op jit(solution)/shard_map/ppermute | solution.py:18
  239.4 10.1 %collective-permute-start.6 = (f32[8,512]{1,0:T(8,128)S(1)}, f32[8,512]{1,0:T(8,128)S(1)}, u32[]{:S(2)}, u32[]{:S(2)}) collective-permute-start(f32[8,512]{1,0:T(8,128)S(1)} %get-tuple-element.187), channel_id=1, source_target_pairs={{0,1},{1,2},{2,3},{3,4},{4,5},{5,6},{6,7},{7,8},{8,9},{9,10},{10,1... | collective-permute-start | bytes 49160 | tf_op jit(solution)/shard_map/ppermute | solution.py:18
  239.8 18.3 %collective-permute-start.7 = (f32[8,512]{1,0:T(8,128)S(1)}, f32[8,512]{1,0:T(8,128)S(1)}, u32[]{:S(2)}, u32[]{:S(2)}) collective-permute-start(f32[8,512]{1,0:T(8,128)S(1)} %get-tuple-element.186), channel_id=1, source_target_pairs={{0,31},{1,0},{2,1},{3,2},{4,3},{5,4},{6,5},{7,6},{8,7},{9,8},{10,9... | collective-permute-start | bytes 49160 | tf_op jit(solution)/shard_map/ppermute | solution.py:18
  244.8 13.4 %collective-permute-start.8 = (f32[8,512]{1,0:T(8,128)S(1)}, f32[8,512]{1,0:T(8,128)S(1)}, u32[]{:S(2)}, u32[]{:S(2)}) collective-permute-start(f32[8,512]{1,0:T(8,128)S(1)} %get-tuple-element.185), channel_id=1, source_target_pairs={{0,4},{1,5},{2,6},{3,7},{4,8},{5,9},{6,10},{7,11},{8,12},{9,13},{1... | collective-permute-start | bytes 49160 | tf_op jit(solution)/shard_map/ppermute | solution.py:18
  244.8 13.4 %collective-permute-start.9 = (f32[8,512]{1,0:T(8,128)S(1)}, f32[8,512]{1,0:T(8,128)S(1)}, u32[]{:S(2)}, u32[]{:S(2)}) collective-permute-start(f32[8,512]{1,0:T(8,128)S(1)} %get-tuple-element.184), channel_id=1, source_target_pairs={{0,28},{1,29},{2,30},{3,31},{4,0},{5,1},{6,2},{7,3},{8,4},{9,5},{1... | collective-permute-start | bytes 49160 | tf_op jit(solution)/shard_map/ppermute | solution.py:18
  249.5 13.4 %collective-permute-start.10 = (f32[8,512]{1,0:T(8,128)S(1)}, f32[8,512]{1,0:T(8,128)S(1)}, u32[]{:S(2)}, u32[]{:S(2)}) collective-permute-start(f32[8,512]{1,0:T(8,128)S(1)} %get-tuple-element.183), channel_id=1, source_target_pairs={{0,16},{1,17},{2,18},{3,19},{4,20},{5,21},{6,22},{7,23},{8,24},{9,... | collective-permute-start | bytes 49160 | tf_op jit(solution)/shard_map/ppermute | solution.py:18
  258.1 8.3 collective-permute-start.14
  258.2 8.9 collective-permute-start.15
  394.4 10.1 %collective-permute-start.18 = (f32[8,512]{1,0:T(8,128)S(1)}, f32[8,512]{1,0:T(8,128)S(1)}, u32[]{:S(2)}, u32[]{:S(2)}) collective-permute-start(f32[8,512]{1,0:T(8,128)S(1)} %get-tuple-element.181), channel_id=1, source_target_pairs={{0,1},{1,2},{2,3},{3,4},{4,5},{5,6},{6,7},{7,8},{8,9},{9,10},{10,1... | collective-permute-start | bytes 49160 | tf_op jit(solution)/shard_map/ppermute | solution.py:18
  394.5 13.6 %collective-permute-start.19 = (f32[8,512]{1,0:T(8,128)S(1)}, f32[8,512]{1,0:T(8,128)S(1)}, u32[]{:S(2)}, u32[]{:S(2)}) collective-permute-start(f32[8,512]{1,0:T(8,128)S(1)} %get-tuple-element.180), channel_id=1, source_target_pairs={{0,31},{1,0},{2,1},{3,2},{4,3},{5,4},{6,5},{7,6},{8,7},{9,8},{10,9... | collective-permute-start | bytes 49160 | tf_op jit(solution)/shard_map/ppermute | solution.py:18
  399.8 8.9 collective-permute-start.20
  399.8 9.5 collective-permute-start.21
  601.3 10.3 %collective-permute-start.24 = (f32[8,512]{1,0:T(8,128)S(1)}, f32[8,512]{1,0:T(8,128)S(1)}, u32[]{:S(2)}, u32[]{:S(2)}) collective-permute-start(f32[8,512]{1,0:T(8,128)S(1)} %get-tuple-element.175), channel_id=1, source_target_pairs={{0,1},{1,2},{2,3},{3,4},{4,5},{5,6},{6,7},{7,8},{8,9},{9,10},{10,1... | collective-permute-start | bytes 49160 | tf_op jit(solution)/shard_map/ppermute | solution.py:18
  601.6 13.6 %collective-permute-start.25 = (f32[8,512]{1,0:T(8,128)S(1)}, f32[8,512]{1,0:T(8,128)S(1)}, u32[]{:S(2)}, u32[]{:S(2)}) collective-permute-start(f32[8,512]{1,0:T(8,128)S(1)} %get-tuple-element.174), channel_id=1, source_target_pairs={{0,31},{1,0},{2,1},{3,2},{4,3},{5,4},{6,5},{7,6},{8,7},{9,8},{10,9... | collective-permute-start | bytes 49160 | tf_op jit(solution)/shard_map/ppermute | solution.py:18
  606.9 8.9 collective-permute-start.26
  606.9 9.5 collective-permute-start.27
  809.7 10.1 %collective-permute-start.30 = (f32[8,512]{1,0:T(8,128)S(1)}, f32[8,512]{1,0:T(8,128)S(1)}, u32[]{:S(2)}, u32[]{:S(2)}) collective-permute-start(f32[8,512]{1,0:T(8,128)S(1)} %get-tuple-element.169), channel_id=1, source_target_pairs={{0,1},{1,2},{2,3},{3,4},{4,5},{5,6},{6,7},{7,8},{8,9},{9,10},{10,1... | collective-permute-start | bytes 49160 | tf_op jit(solution)/shard_map/ppermute | solution.py:18
  809.8 13.6 %collective-permute-start.31 = (f32[8,512]{1,0:T(8,128)S(1)}, f32[8,512]{1,0:T(8,128)S(1)}, u32[]{:S(2)}, u32[]{:S(2)}) collective-permute-start(f32[8,512]{1,0:T(8,128)S(1)} %get-tuple-element.168), channel_id=1, source_target_pairs={{0,31},{1,0},{2,1},{3,2},{4,3},{5,4},{6,5},{7,6},{8,7},{9,8},{10,9... | collective-permute-start | bytes 49160 | tf_op jit(solution)/shard_map/ppermute | solution.py:18
  815.1 8.9 collective-permute-start.32
  815.1 9.5 collective-permute-start.33
  (94 other events, 3326.3 us)
